TPU v7x, 256 devices: a whole 4x4x8 slice. The times are simulated.
256 devices in a mesh: dp: 32 (over y, z), group: 8 (over x, core).
Axes of the slice: x: 4, y: 4, z: 8, core: 2. Of those that a mesh axis runs over, the one named last changes fastest.
Arguments:
- keys: int32 [131072], P(('dp', 'group')), may hold values from 0 to 1073741823
- cut: int32 [1], replicated, may hold values from 256 to 1023
- owner: int32 [131072, 1], P(('dp', 'group')), may hold values from 0 to 31; in each aligned block of 512 rows (0 to 511, 512 to 1023, ...) at most 32 rows name the same one
- tokens: int32 [131072, 2048], P(('dp', 'group')), may hold values from 0 to 128255
Outputs:
- histogram: int32 [4096], replicated
- packed_rows: int32 [262144, 2048], P(('dp', 'group'))
- packed_weights: float32 [262144], P(('dp', 'group'))
Inputs may be any that keep to these rules, and one draw needn't show every extreme that they name: Among the examples of one device, at most 32 have the same owner, and some owner has exactly 32.
All inputs are finite; a program needn't handle non-finite values.
Results may differ from a plain program's by a relative error of at most 0.0003.
Values sent between devices are 32-bit elements; how exact they have to be, the bound alone decides.
A program may use at most 128 MiB of HBM per device.

v0:
```python
import jax
import jax.numpy as jnp
from jax import lax
from jax.sharding import Mesh
from jax.sharding import PartitionSpec as P

BINS = 4096
BIN_WIDTH = 262144
DP = ("dp_0", "dp_1")
GROUP = ("group_0", "group_1")
DP_GROUP = ("dp_0", "dp_1", "group_0", "group_1")


def neutral_like(value, identity):
    return jnp.broadcast_to(jnp.asarray(identity, value.dtype), value.shape)


def prefix_by_axis(value, axes, combine, identity):
    before = start = neutral_like(value, identity)
    so_far = value
    for axis in reversed(axes):
        count, index = (lax.axis_size(axis), lax.axis_index(axis))
        pieces = lax.all_gather(so_far, axis)
        inside, so_far = (start, start)
        for k in range(count):
            passed = k < index
            so_far = combine(so_far, pieces[k])
            inside = jnp.where(passed, so_far, inside)
        before = combine(inside, before)
    return before


def split_up(value, dim, count):
    before, after = (value.shape[:dim], value.shape[dim + 1 :])
    return jnp.moveaxis(value.reshape(*before, count, -1, *after), dim, 0)


def laid_out(tiles, dim):
    tiles = jnp.moveaxis(tiles, 0, dim)
    dims = tiles.shape
    return tiles.reshape(*dims[:dim], dims[dim] * dims[dim + 1], *dims[dim + 2 :])


def exchange_both(value, axis, axes, splits, concats):
    sizes = [lax.axis_size(a) for a in axes]
    tiles = split_up(value, splits[0], sizes[0])
    tiles = jnp.moveaxis(split_up(tiles, splits[1] + 1, sizes[1]), 0, 1)
    inside = tiles.shape[2:]
    tiles = tiles.reshape(-1, *inside)
    tiles = lax.all_to_all(tiles, axis, split_axis=0, concat_axis=0, tiled=True)
    tiles = laid_out(tiles.reshape(*sizes, *inside), concats[0] + 1)
    return laid_out(tiles, concats[1])


def add_counts(earlier, later):
    return earlier + later


def body(keys, cut, owner, tokens):
    examples = keys.shape[0]
    width = tokens.shape[1]
    n_owner = lax.axis_size(DP)
    n_member = lax.axis_size(GROUP)
    slots = 2 * examples // (n_owner * n_member)
    capacity = 2 * examples
    bins_of = keys // BIN_WIDTH
    local_hist = jnp.zeros((BINS,), jnp.float32).at[bins_of].add(1.0)
    kept = bins_of >= cut[0]
    dest = owner[:, 0]
    onehot = (
        (dest[:, None] == jnp.arange(n_owner, dtype=jnp.int32)[None, :]) & kept[:, None]
    ).astype(jnp.int32)
    counts = jnp.sum(onehot, axis=0).astype(jnp.float32)
    before = prefix_by_axis(counts, DP_GROUP, add_counts, jnp.zeros_like(counts))
    hist = lax.psum(local_hist, DP_GROUP)
    running = jnp.cumsum(onehot, axis=0) - onehot
    local_rank = jnp.sum(running * onehot, axis=1)
    offset = jnp.sum(before.astype(jnp.int32)[None, :] * onehot, axis=1)
    rank = offset + local_rank
    member = rank % n_member
    outside = n_owner * n_member * slots
    position_send = jnp.where(
        kept, (dest * n_member + member) * slots + local_rank // n_member, outside
    )
    send_rows = jnp.zeros((outside, width), jnp.int32).at[position_send].set(tokens, mode="drop")
    details = jnp.stack([rank // n_member, keys], axis=1)
    send_meta = jnp.full((outside, 2), -1, jnp.int32).at[position_send].set(details, mode="drop")
    send_rows = send_rows.reshape(n_owner, n_member, slots, width)
    send_meta = send_meta.reshape(n_owner, n_member, slots, 2)
    got_rows, got_meta = (
        exchange_both(send_rows, DP_GROUP, (DP, GROUP), (0, 1), (0, 1)),
        exchange_both(send_meta, DP_GROUP, (DP, GROUP), (0, 1), (0, 1)),
    )
    got_rows = got_rows.reshape(-1, width)
    got_meta = got_meta.reshape(-1, 2)
    slot = got_meta[:, 0]
    valid = slot >= 0
    target = jnp.where(valid, slot, capacity)
    suffix = jnp.cumsum(hist[::-1])[::-1]
    total = jnp.maximum(suffix[cut[0]], 1.0)
    got_bins = jnp.clip(got_meta[:, 1] // BIN_WIDTH, 0, BINS - 1)
    weight = jnp.where(valid, suffix[got_bins] / total, 0.0)
    packed_rows = jnp.zeros((capacity, width), jnp.int32).at[target].set(got_rows, mode="drop")
    packed_weights = jnp.zeros((capacity,), jnp.float32).at[target].set(weight, mode="drop")
    return (hist.astype(jnp.int32), packed_rows, packed_weights)


def solution(mesh):
    torus = Mesh(mesh.devices.reshape(4, 8, 4, 2), ("dp_0", "dp_1", "group_0", "group_1"))
    placed = (P(DP_GROUP), P(), P(DP_GROUP, None), P(DP_GROUP, None))
    return jax.shard_map(
        body,
        mesh=torus,
        in_specs=placed,
        out_specs=(P(), P(DP_GROUP, None), P(DP_GROUP)),
        check_vma=False,
    )
```

profile of v0, /device:TPU:1, one launch (start us, length us, event | category | flops | bytes accessed | tf_op | source)
XLA Modules:
  0.0 360.7 jit_solution(18366167405808590215)
XLA Ops:
  1.3 0.7 broadcast_compare_fusion
  2.0 0.8 convert_reduce_fusion
  2.8 1.3 dynamic-slice
  4.8 5.3 %all-reduce = f32[64]{0:T(128)S(1)} all-reduce(f32[64]{0:T(128)S(1)} %convert_dynamic-update-slice_fusion), channel_id=2, replica_groups=mesh['dp_0'=4,'dp_1'=8,'group_0'=4,'group_1'=2] {'group_1'}, use_global_device_ids=true, to_apply=%add | all-reduce | flops 64 | bytes 512
  10.1 1.3 dynamic-slice.1
  12.2 6.7 %all-reduce.1 = f32[128]{0:T(128)S(1)} all-reduce(f32[128]{0:T(128)S(1)} %fusion.35), channel_id=3, replica_groups=mesh['dp_0'=4,'dp_1'=8,'group_0'=4,'group_1'=2] {'group_0'}, use_global_device_ids=true, to_apply=%add.1 | all-reduce | flops 128 | bytes 1024
  19.0 15.4 %all-gather.2 = f32[8,1,32]{2,1,0:T(1,128)S(1)} all-gather(f32[1,1,32]{2,1,0:T(1,128)S(1)} %fusion.37), channel_id=1, replica_groups=mesh['dp_0'=4,'dp_1'=8,'group_0'=4,'group_1'=2] {'dp_1'}, dimensions={0}, use_global_device_ids=true | all-gather | bytes 1152 | tf_op jit(solution)/shard_map/all_gather | solution.py:23
  34.4 7.9 %all-gather.3 = f32[4,1,32]{2,1,0:T(1,128)S(1)} all-gather(f32[1,1,32]{2,1,0:T(1,128)S(1)} %bitcast.115), channel_id=1, replica_groups=mesh['dp_0'=4,'dp_1'=8,'group_0'=4,'group_1'=2] {'dp_0'}, dimensions={0}, use_global_device_ids=true | all-gather | bytes 640 | tf_op jit(solution)/shard_map/all_gather | solution.py:23
  42.4 0.7 fusion.10
  43.1 1.2 reduce-window.15
  44.6 0.8 select_reduce_fusion
  45.4 0.7 compare_select_fusion.6
  47.0 1.8 scatter_custom_fusion.1
  48.8 2.3 copy.14
  51.1 13.2 %all-to-all-start = ((s32[256,1,1,4,2]{3,4,2,1,0:T(2,128)}), s32[256,1,1,4,2]{3,4,2,1,0:T(2,128)S(1)}, u32[]{:S(2)}, u32[]{:S(2)}) async-start(s32[256,1,1,4,2]{3,4,2,1,0:T(2,128)} %copy.14), calls=%async_computation | async-start | bytes 524288 | tf_op jit(solution)/shard_map/all_to_all | solution.py:50
  64.3 8.6 %scatter_custom_fusion.2 = s32[1024,2048]{1,0:T(8,128)} fusion(s32[512]{0:T(512)S(1)} %get-tuple-element.5, s32[512,2048]{1,0:T(8,128)} %param.7, s32[]{:T(128)} %constant.97.clone.1), kind=kCustom, calls=%fused_computation.8 | custom fusion | bytes 8389120 | tf_op jit(solution)/shard_map/scatter | solution.py:85
  72.9 9.8 %reshape_transpose_transpose_reshape_reshape_reshape.7 = s32[256,1,1,4,2048]{4,3,0,2,1:T(4,128)} reshape(s32[1024,2048]{1,0:T(8,128)} %scatter_custom_fusion.2) | data formatting | bytes 16777216 | tf_op jit(solution)/shard_map/reshape;transpose;transpose;reshape;reshape;reshape | solution.py:49
  82.7 14.9 %all-to-all-start.1 = ((s32[256,1,1,4,2048]{4,3,2,1,0:T(4,128)}), s32[256,1,1,4,2048]{4,3,2,1,0:T(4,128)}, u32[]{:S(2)}, u32[]{:S(2)}) async-start(s32[256,1,1,4,2048]{4,3,2,1,0:T(4,128)} %bitcast.102), calls=%async_computation.1 | async-start | bytes 16777216 | tf_op jit(solution)/shard_map/all_to_all | solution.py:50
  97.6 3.3 scatter_custom_fusion
  100.8 222.9 %psum.7 = f32[4096]{0:T(1024)S(1)} all-reduce(f32[4096]{0:T(1024)S(1)} %scatter_custom_fusion), channel_id=1, replica_groups=mesh['dp_0'=4,'dp_1'=8,'group_0'=4,'group_1'=2] {'dp_0','dp_1','group_0'..., use_global_device_ids=true, to_apply=%region_1.2 | all-reduce | flops 4096 | bytes 32768 | tf_op jit(solution)/shard_map/psum | solution.py:75
  326.6 6.2 %gather_fusion = f32[1024]{0:T(1024)S(1)} fusion(f32[4096]{0:T(1024)S(1)} %rev.7, s32[1024]{0:T(1024)S(1)} %broadcast_clamp_fusion), kind=kCustom, calls=%fused_computation | custom fusion | bytes 12288 | tf_op jit(solution)/shard_map/gather | solution.py:102
  332.8 4.9 %scatter_custom_fusion.4 = f32[1024]{0:T(1024)} fusion(s32[1024]{0:T(1024)S(1)} %bitcast.116, f32[1024]{0:T(1024)S(1)} %divide_select_fusion, f32[]{:T(128)} %constant.95.clone.1), kind=kCustom, calls=%fused_computation.65 | custom fusion | bytes 4100 | tf_op jit(solution)/shard_map/scatter | solution.py:104
  337.7 10.0 %reshape.165 = s32[1024,2048]{1,0:T(8,128)} reshape(s32[32,8,1,4,2048]{4,3,1,0,2:T(4,128)} %bitcast.31) | data formatting | bytes 16777216 | tf_op jit(solution)/shard_map/reshape;reshape | solution.py:94
  347.7 13.0 %scatter_custom_fusion.3 = s32[1024,2048]{1,0:T(8,128)} fusion(s32[1024]{0:T(1024)S(1)} %bitcast.117, s32[1024,2048]{1,0:T(8,128)} %reshape.165, s32[]{:T(128)} %constant.97.clone.1), kind=kCustom, calls=%fused_computation.6 | custom fusion | bytes 8389120 | tf_op jit(solution)/shard_map/scatter | solution.py:103
  (32 shorter events, 3.8 us)
Async XLA Ops:
  51.1 31.6 %all-to-all-start = ((s32[256,1,1,4,2]{3,4,2,1,0:T(2,128)}), s32[256,1,1,4,2]{3,4,2,1,0:T(2,128)S(1)}, u32[]{:S(2)}, u32[]{:S(2)}) async-start(s32[256,1,1,4,2]{3,4,2,1,0:T(2,128)} %copy.14), calls=%async_computation | async-start | bytes 524288 | tf_op jit(solution)/shard_map/all_to_all | solution.py:50
  82.7 255.0 %all-to-all-start.1 = ((s32[256,1,1,4,2048]{4,3,2,1,0:T(4,128)}), s32[256,1,1,4,2048]{4,3,2,1,0:T(4,128)}, u32[]{:S(2)}, u32[]{:S(2)}) async-start(s32[256,1,1,4,2048]{4,3,2,1,0:T(4,128)} %bitcast.102), calls=%async_computation.1 | async-start | bytes 16777216 | tf_op jit(solution)/shard_map/all_to_all | solution.py:50
where the time goes:
time: 362 us; the launch traced here: 361 us
  blocking collectives  258 us (71%)
  local copies, waits for them, and re-layouts  60.7 us (17%)
  starting transfers between devices  28 us (8%)
  other arithmetic  10.4 us (3%)
    psum x1, blocking collectives, body(): hist = lax.psum(local_hist, DP_GROUP)  223 us
    all_to_all x2, starting transfers between devices, exchange_both(): tiles = lax.all_to_all(tiles, axis, split_axis=0, concat_axis=0, tiled=True)  28 us
    all_gather x2, blocking collectives, prefix_by_axis(): pieces = lax.all_gather(so_far, axis)  23.3 us
    scatter x1, local copies, waits for them, and re-layouts, body(): jnp.zeros((capacity, width), jnp.int32).at[target]  13 us
    another operation x2, local copies, waits for them, and re-layouts, exchange_both(): tiles = tiles.reshape(-1, *inside)  12.1 us
    unnamed x2, blocking collectives  12 us
    another operation x1, local copies, waits for them, and re-layouts, body(): got_rows = got_rows.reshape(-1, width)  10 us
    scatter x1, local copies, waits for them, and re-layouts, body(): jnp.zeros((outside, width), jnp.int32).at[position_send]  8.6 us
  transfers between devices with their start and end apart: 2, of which 0 were waited for; matrix products, arithmetic and copies ran while one was open for 10% of the time, Pallas kernels for 0%

commit v1 on v0

--- a/solution.py
+++ b/solution.py
@@ -1,3 +1,4 @@
+import functools
 import jax
 import jax.numpy as jnp
 from jax import lax
@@ -9,6 +10,13 @@
 DP = ("dp_0", "dp_1")
 GROUP = ("group_0", "group_1")
 DP_GROUP = ("dp_0", "dp_1", "group_0", "group_1")
+
+
+def review_goods(my_data, chip_axis):
+    return jnp.sum(lax.all_gather(my_data, axis_name=chip_axis), 0)
+
+
+update_the_stops_all = functools.partial(review_goods, chip_axis=DP_GROUP)
 
 
 def neutral_like(value, identity):
@@ -72,7 +80,7 @@
     ).astype(jnp.int32)
     counts = jnp.sum(onehot, axis=0).astype(jnp.float32)
     before = prefix_by_axis(counts, DP_GROUP, add_counts, jnp.zeros_like(counts))
-    hist = lax.psum(local_hist, DP_GROUP)
+    hist = update_the_stops_all(local_hist)
     running = jnp.cumsum(onehot, axis=0) - onehot
     local_rank = jnp.sum(running * onehot, axis=1)
     offset = jnp.sum(before.astype(jnp.int32)[None, :] * onehot, axis=1)

time: 362 us -> 332 us (0.917)
  blocking collectives: 258 us -> 35.4 us
  waiting for transfers between devices: 0.01 us -> 172 us
  between operations: 3.41 us -> 16.8 us
  local copies, waits for them, and re-layouts: 60.7 us -> 65.6 us
    psum x1 -> x0, blocking collectives: 223 us -> none  [body(): hist = lax.psum(local_hist, DP_GROUP)]
    all_gather x0 -> x1, waiting for transfers between devices: none -> 137 us  [review_goods(): return jnp.sum(lax.all_gather(my_data, axis_name=chip_axis), 0)]
    all_to_all x2, waiting for transfers between devices: 0.01 us -> 34.3 us  [exchange_both(): tiles = lax.all_to_all(tiles, axis, split_axis=0, concat_axis=0, tiled=True)]
    all_gather x0 -> x1, local copies, waits for them, and re-layouts: none -> 4.94 us  [review_goods(): return jnp.sum(lax.all_gather(my_data, axis_name=chip_axis), 0)]
  transfers between devices with their start and end apart: 2 -> 3, of which waited for: 0 -> 2; matrix products, arithmetic and copies ran while one was open for 10% -> 13% of each run, Pallas kernels for 0% -> 0%
where the time goes in v1:
time: 332 us; the launch traced here: 331 us
  waiting for transfers between devices  172 us (52%)
  local copies, waits for them, and re-layouts  65.6 us (20%)
  blocking collectives  35.4 us (11%)
  starting transfers between devices  28.1 us (8%)
  between operations  16.8 us (5%)
  other arithmetic  13.3 us (4%)
    all_gather x1, waiting for transfers between devices, review_goods(): return jnp.sum(lax.all_gather(my_data, axis_name=chip_axis), 0)  137 us
    all_to_all x2, waiting for transfers between devices, exchange_both(): tiles = lax.all_to_all(tiles, axis, split_axis=0, concat_axis=0, tiled=True)  34.3 us
    all_to_all x2, starting transfers between devices, exchange_both(): tiles = lax.all_to_all(tiles, axis, split_axis=0, concat_axis=0, tiled=True)  28 us
    all_gather x2, blocking collectives, prefix_by_axis(): pieces = lax.all_gather(so_far, axis)  23.3 us
    scatter x1, local copies, waits for them, and re-layouts, body(): jnp.zeros((capacity, width), jnp.int32).at[target]  13 us
    another operation x2, local copies, waits for them, and re-layouts, exchange_both(): tiles = tiles.reshape(-1, *inside)  12.1 us
    unnamed x2, blocking collectives  12 us
    another operation x1, local copies, waits for them, and re-layouts, body(): got_rows = got_rows.reshape(-1, width)  10 us
  transfers between devices with their start and end apart: 3, of which 2 were waited for; matrix products, arithmetic and copies ran while one was open for 13% of the time, Pallas kernels for 0%

profile of v1, /device:TPU:1, one launch (start us, length us, event | category | flops | bytes accessed | tf_op | source)
XLA Modules:
  0.0 330.8 jit_solution(4825490791358095705)
XLA Ops:
  8.5 0.8 convert_reduce_fusion
  9.3 1.3 dynamic-slice
  11.4 5.3 %all-reduce = f32[64]{0:T(128)S(1)} all-reduce(f32[64]{0:T(128)S(1)} %convert_dynamic-update-slice_fusion), channel_id=3, replica_groups=mesh['dp_0'=4,'dp_1'=8,'group_0'=4,'group_1'=2] {'group_1'}, use_global_device_ids=true, to_apply=%add | all-reduce | flops 64 | bytes 512
  16.7 1.3 dynamic-slice.1
  18.8 6.7 %all-reduce.1 = f32[128]{0:T(128)S(1)} all-reduce(f32[128]{0:T(128)S(1)} %fusion.35), channel_id=4, replica_groups=mesh['dp_0'=4,'dp_1'=8,'group_0'=4,'group_1'=2] {'group_0'}, use_global_device_ids=true, to_apply=%add.1 | all-reduce | flops 128 | bytes 1024
  25.6 15.4 %all-gather.3 = f32[8,1,32]{2,1,0:T(1,128)S(1)} all-gather(f32[1,1,32]{2,1,0:T(1,128)S(1)} %fusion.37), channel_id=1, replica_groups=mesh['dp_0'=4,'dp_1'=8,'group_0'=4,'group_1'=2] {'dp_1'}, dimensions={0}, use_global_device_ids=true | all-gather | bytes 1152 | tf_op jit(solution)/shard_map/all_gather | solution.py:31
  41.0 7.9 %all-gather.4 = f32[4,1,32]{2,1,0:T(1,128)S(1)} all-gather(f32[1,1,32]{2,1,0:T(1,128)S(1)} %bitcast.115), channel_id=1, replica_groups=mesh['dp_0'=4,'dp_1'=8,'group_0'=4,'group_1'=2] {'dp_0'}, dimensions={0}, use_global_device_ids=true | all-gather | bytes 640 | tf_op jit(solution)/shard_map/all_gather | solution.py:31
  49.6 1.2 reduce-window.15
  51.1 0.8 select_reduce_fusion
  53.5 1.8 scatter_custom_fusion.1
  55.3 2.3 copy.20
  57.6 13.2 %all-to-all-start = ((s32[256,1,1,4,2]{3,4,2,1,0:T(2,128)}), s32[256,1,1,4,2]{3,4,2,1,0:T(2,128)S(1)}, u32[]{:S(2)}, u32[]{:S(2)}) async-start(s32[256,1,1,4,2]{3,4,2,1,0:T(2,128)} %copy.20), calls=%async_computation | async-start | bytes 524288 | tf_op jit(solution)/shard_map/all_to_all | solution.py:58
  70.8 8.6 %scatter_custom_fusion.2 = s32[1024,2048]{1,0:T(8,128)} fusion(s32[512]{0:T(512)S(1)} %get-tuple-element.5, s32[512,2048]{1,0:T(8,128)} %param.7, s32[]{:T(128)} %constant.97.clone.1), kind=kCustom, calls=%fused_computation.8 | custom fusion | bytes 8389120 | tf_op jit(solution)/shard_map/scatter | solution.py:93
  79.4 9.8 %reshape_transpose_transpose_reshape_reshape_reshape.7 = s32[256,1,1,4,2048]{4,3,0,2,1:T(4,128)} reshape(s32[1024,2048]{1,0:T(8,128)} %scatter_custom_fusion.2) | data formatting | bytes 16777216 | tf_op jit(solution)/shard_map/reshape;transpose;transpose;reshape;reshape;reshape | solution.py:57
  89.2 14.9 %all-to-all-start.1 = ((s32[256,1,1,4,2048]{4,3,2,1,0:T(4,128)}), s32[256,1,1,4,2048]{4,3,2,1,0:T(4,128)}, u32[]{:S(2)}, u32[]{:S(2)}) async-start(s32[256,1,1,4,2048]{4,3,2,1,0:T(4,128)} %bitcast.102), calls=%async_computation.1 | async-start | bytes 16777216 | tf_op jit(solution)/shard_map/all_to_all | solution.py:58
  104.1 3.8 %scatter_custom_fusion = f32[4096]{0:T(1024)} fusion(s32[512]{0:T(512)S(1)} %compare_select_fusion.7, f32[512]{0:T(512)S(1)} %broadcast.158, f32[]{:T(128)} %constant.95.clone.1), kind=kCustom, calls=%fused_computation.36 | custom fusion | flops 512 | bytes 16388 | tf_op jit(solution)/shard_map/scatter-add | solution.py:75
  108.3 137.4 %all-gather.7.cloned.1.call-done = f32[1048576]{0:T(1024)} async-done(((f32[4096]{0:T(1024)}), f32[1048576]{0:T(1024)}) %all-gather.7.cloned.1.call-update) | async-done | bytes 4194320 | tf_op jit(solution)/shard_map/all_gather | solution.py:16
  245.7 4.9 %reshape.177 = f32[256,4096]{1,0:T(8,128)} reshape(f32[1048576]{0:T(1024)} %all-gather.7.cloned.1.call-done) | data formatting | bytes 8388608 | tf_op jit(solution)/shard_map/all_gather | solution.py:16
  250.6 2.4 reduce_sum.36
  254.4 6.2 %gather_fusion = f32[1024]{0:T(1024)S(1)} fusion(f32[4096]{0:T(1024)S(1)} %rev.7, s32[1024]{0:T(1024)S(1)} %broadcast_clamp_fusion), kind=kCustom, calls=%fused_computation | custom fusion | bytes 12288 | tf_op jit(solution)/shard_map/gather | solution.py:110
  261.8 4.9 %scatter_custom_fusion.4 = f32[1024]{0:T(1024)} fusion(s32[1024]{0:T(1024)S(1)} %bitcast.116, f32[1024]{0:T(1024)S(1)} %divide_select_fusion, f32[]{:T(128)} %constant.95.clone.1), kind=kCustom, calls=%fused_computation.65 | custom fusion | bytes 4100 | tf_op jit(solution)/shard_map/scatter | solution.py:112
  266.7 34.3 %all-to-all-done.1 = s32[256,1,1,4,2048]{4,3,2,1,0:T(4,128)} async-done(((s32[256,1,1,4,2048]{4,3,2,1,0:T(4,128)}), s32[256,1,1,4,2048]{4,3,2,1,0:T(4,128)}, u32[]{:S(2)}, u32[]{:S(2)}) %all-to-all-start.1) | async-done | bytes 8388640 | tf_op jit(solution)/shard_map/all_to_all | solution.py:58
  300.9 10.0 %reshape.165 = s32[1024,2048]{1,0:T(8,128)} reshape(s32[32,8,1,4,2048]{4,3,1,0,2:T(4,128)} %bitcast.31) | data formatting | bytes 16777216 | tf_op jit(solution)/shard_map/reshape;reshape | solution.py:102
  311.0 13.0 %scatter_custom_fusion.3 = s32[1024,2048]{1,0:T(8,128)} fusion(s32[1024]{0:T(1024)S(1)} %bitcast.117, s32[1024,2048]{1,0:T(8,128)} %reshape.165, s32[]{:T(128)} %constant.97.clone.1), kind=kCustom, calls=%fused_computation.6 | custom fusion | bytes 8389120 | tf_op jit(solution)/shard_map/scatter | solution.py:111
  (36 shorter events, 5.9 us)
Async XLA Ops:
  57.6 31.6 %all-to-all-start = ((s32[256,1,1,4,2]{3,4,2,1,0:T(2,128)}), s32[256,1,1,4,2]{3,4,2,1,0:T(2,128)S(1)}, u32[]{:S(2)}, u32[]{:S(2)}) async-start(s32[256,1,1,4,2]{3,4,2,1,0:T(2,128)} %copy.20), calls=%async_computation | async-start | bytes 524288 | tf_op jit(solution)/shard_map/all_to_all | solution.py:58
  89.2 211.7 %all-to-all-start.1 = ((s32[256,1,1,4,2048]{4,3,2,1,0:T(4,128)}), s32[256,1,1,4,2048]{4,3,2,1,0:T(4,128)}, u32[]{:S(2)}, u32[]{:S(2)}) async-start(s32[256,1,1,4,2048]{4,3,2,1,0:T(4,128)} %bitcast.102), calls=%async_computation.1 | async-start | bytes 16777216 | tf_op jit(solution)/shard_map/all_to_all | solution.py:58
  104.1 141.6 %all-gather.7.cloned.1.call-start = ((), (), s32[]{:S(2)}) async-start(), calls=%async_computation.2 | async-start | bytes 4210688 | tf_op jit(solution)/shard_map/all_gather | solution.py:16
Sparse Core Ops, SparseCore 0:
  109.0 136.5 all-gather.6
